TPU v7x, 32 devices: a whole 2x2x4 slice. The times are simulated.
32 devices in a mesh: parts: 2 (over x), shot: 2 (over core), space: 8 (over z, y).
Axes of the slice: x: 2, y: 2, z: 4, core: 2. Of those that a mesh axis runs over, the one named last changes fastest.
Arguments:
- image: float32 [3200, 2, 192], P(('parts', 'space')), parts along dimension 0, may hold values from -6 to 6
- coil_maps: bfloat16 [16, 3200, 2, 192], P(None, ('parts', 'space')), parts along dimension 1, may hold values from -1.5 to 1.5
- psf_phase: float32 [3200, 576], P(('parts', 'space')), parts along dimension 0, may hold values from -3.140625 to 3.140625
- line_mask: int32 [4, 200], P(('parts', 'shot')), parts along dimension 0, may hold values 0 or 1
- motion: int32 [4, 3], P(('parts', 'shot')), parts along dimension 0, may hold values from 0 to 16
Outputs:
- result: float32 [3200, 2, 192], P(('parts', 'space')), parts along dimension 0
There are 2 independent parts, one for each index of `parts`. A program takes and returns all parts, laid end to end along the dimension named above; each array names one. Nothing has to cross between parts.
Inputs may be any that keep to these rules, and one draw needn't show every extreme that they name: `motion`: column 0 selects the rotation angle, columns 1 and 2 the shifts along x and y.
All inputs are finite; a program needn't handle non-finite values. No bound on the sum of `line_mask` on one device may be relied on, other than what follows from the above.
Results may differ from a plain program's by a relative error of at most 0.003.
Values may be sent and summed in bfloat16 or wider, within the bound.
A program may use at most 64 MiB of HBM per device.

v0:
```python
import functools
import math

import jax
import jax.numpy as jnp
import numpy as np
from jax import lax
from jax.experimental import pallas as pl
from jax.experimental.pallas import tpu as pltpu
from jax.sharding import PartitionSpec as P

NY = 200
LEVELS = 17


PRECISE = lax.Precision.HIGHEST
ANGLE_STEP = 0.02
SHIFT_STEP = 0.5


def from_partner(value, axis, apart):
    mask = 2**apart
    pairs = [(source, source ^ mask) for source in range(lax.axis_size(axis))]
    return lax.ppermute(value, axis, pairs)


def dft_parts(size_in, size_out, modulus, sign):
    inputs = jnp.arange(size_in, dtype=jnp.int32)[:, None]
    outputs = jnp.arange(size_out, dtype=jnp.int32)[None, :]
    angle = (inputs * outputs % modulus).astype(jnp.float32) * (2.0 * jnp.pi / modulus)
    factor = float(modulus) ** (-0.5)
    return (jnp.cos(angle) * factor, jnp.sin(angle) * (sign * factor))


def block(parts):
    real_part, imag_part = parts
    upper = jnp.concatenate([real_part, imag_part], 1)
    bottom = jnp.concatenate([-imag_part, real_part], 1)
    return jnp.concatenate([upper, bottom], 0)


def quad(real_part, imag_part):
    return jnp.stack(
        [jnp.stack([real_part, -imag_part], 1), jnp.stack([imag_part, real_part], 1)], 0
    )


def signed_freq(length):
    counter = jnp.arange(length, dtype=jnp.int32)
    return jnp.where(counter < length // 2, counter, counter - length).astype(jnp.float32)


def turn_phase(values, phase):
    cosine = jnp.cos(phase)
    sine_part = jnp.sin(phase)
    real_part = values[..., 0, :]
    imag_part = values[..., 1, :]
    return jnp.stack(
        [real_part * cosine - imag_part * sine_part, real_part * sine_part + imag_part * cosine], -2
    )


def complex_mul(left, right):
    return jnp.stack(
        [
            left[..., 0, :] * right[..., 0, :] - left[..., 1, :] * right[..., 1, :],
            left[..., 0, :] * right[..., 1, :] + left[..., 1, :] * right[..., 0, :],
        ],
        -2,
    )


def conj_mul(left, right):
    return jnp.stack(
        [
            left[..., 0, :] * right[..., 0, :] + left[..., 1, :] * right[..., 1, :],
            left[..., 0, :] * right[..., 1, :] - left[..., 1, :] * right[..., 0, :],
        ],
        -2,
    )


def shear_rows(values, shift, sign):
    length = values.shape[-1]
    lines = values.shape[0]
    forward = block(dft_parts(length, length, length, -1.0))
    inverse = block(dft_parts(length, length, length, 1.0))
    spectra = jnp.dot(
        values.reshape(lines, 2 * length),
        forward,
        precision=PRECISE,
        preferred_element_type=jnp.float32,
    )
    phase = sign * -2.0 * jnp.pi / length * shift[:, None] * signed_freq(length)[None, :]
    spectra = turn_phase(spectra.reshape(lines, 2, length), phase)
    result = jnp.dot(
        spectra.reshape(lines, 2 * length),
        inverse,
        precision=PRECISE,
        preferred_element_type=jnp.float32,
    )
    return result.reshape(lines, 2, length)


def shear_columns(values, shift, sign):
    length = values.shape[1]
    forward = quad(*dft_parts(length, length, length, -1.0))
    inverse = quad(*dft_parts(length, length, length, 1.0))
    spectra = jnp.einsum("oaib,zbix->zaox", forward, values, precision=PRECISE)
    phase = sign * -2.0 * jnp.pi / length * signed_freq(length)[:, None] * shift[None, :]
    spectra = turn_phase(spectra, phase)
    return jnp.einsum("oaib,zbix->zaox", inverse, spectra, precision=PRECISE)


def geometry(motion_row):
    offsets = motion_row.astype(jnp.float32) - (LEVELS - 1) / 2.0
    angle = offsets[0] * ANGLE_STEP
    return (-jnp.tan(angle / 2.0), jnp.sin(angle), offsets[1] * SHIFT_STEP, offsets[2] * SHIFT_STEP)


def line_table(mask_row):
    cosine, sine_part = dft_parts(NY, NY, NY, 1.0)
    weight = mask_row.astype(jnp.float32)[:, None]
    real_part = jnp.dot(cosine.T, weight * cosine, precision=PRECISE) + jnp.dot(
        sine_part.T, weight * sine_part, precision=PRECISE
    )
    imag_part = jnp.dot(sine_part.T, weight * cosine, precision=PRECISE) - jnp.dot(
        cosine.T, weight * sine_part, precision=PRECISE
    )
    return quad(real_part, imag_part).astype(jnp.bfloat16)


def to_columns(values):
    return lax.all_to_all(values, "space", split_axis=2, concat_axis=0, tiled=True)


def to_rows(values):
    return lax.all_to_all(values, "space", split_axis=0, concat_axis=2, tiled=True)


def rotate_shards(values, motion_row, sign, device_rank, devices):
    slope, tilt, shift_x, shift_y = geometry(motion_row)
    lines = values.shape[0]
    width = values.shape[2]
    across = ((device_rank * lines + jnp.arange(lines, dtype=jnp.int32)) % NY).astype(
        jnp.float32
    ) - NY / 2.0

    def column_pass(current):
        columns = width // devices
        along = (device_rank * columns + jnp.arange(columns, dtype=jnp.int32)).astype(
            jnp.float32
        ) - width / 2.0
        gathered = to_columns(current)
        all_lines = gathered.shape[0]
        view_slices = gathered.reshape(all_lines // NY, NY, 2, columns)
        sheared = shear_columns(view_slices, tilt * along + shift_y, sign).reshape(
            all_lines, 2, columns
        )
        return to_rows(sheared)

    if sign > 0:
        current = shear_rows(values, slope * across + shift_x, 1.0)
        current = column_pass(current)
        return shear_rows(current, slope * across, 1.0)
    current = shear_rows(values, slope * across, -1.0)
    current = column_pass(current)
    return shear_rows(current, slope * across + shift_x, -1.0)


def gather_slice(values, bit_count, device_rank):
    for bit_index in range(bit_count):
        partner = from_partner(values, "space", bit_index)
        low_side = device_rank >> bit_index & 1 == 0
        values = jnp.where(
            low_side, jnp.concatenate([values, partner], 0), jnp.concatenate([partner, values], 0)
        )
    return values


def sum_slice(values, bit_count, device_rank):
    for bit_index in reversed(range(bit_count)):
        half_rows = values.shape[0] // 2
        low_side = device_rank >> bit_index & 1 == 0
        kept_part = jnp.where(low_side, values[:half_rows], values[half_rows:])
        sent_part = jnp.where(low_side, values[half_rows:], values[:half_rows])
        values = kept_part + from_partner(sent_part, "space", bit_index)
    return values


def regroup_coils(coil_maps, bit_count, device_rank):
    group_size = 1 << bit_count
    pieces = coil_maps.reshape((group_size, coil_maps.shape[0] // group_size) + coil_maps.shape[1:])
    for bit_index in range(bit_count):
        old_shape = pieces.shape
        halves = pieces.reshape((group_size >> bit_index + 1, 2, 1 << bit_index) + old_shape[1:])
        low_side = device_rank >> bit_index & 1 == 0
        kept_part = jnp.where(low_side, halves[:, 0], halves[:, 1])
        sent_part = jnp.where(low_side, halves[:, 1], halves[:, 0])
        partner = from_partner(sent_part, "space", bit_index)
        pieces = jnp.stack(
            [jnp.where(low_side, kept_part, partner), jnp.where(low_side, partner, kept_part)], 1
        ).reshape(old_shape)
    moved = jnp.moveaxis(pieces, 0, 1)
    return moved.reshape((moved.shape[0], group_size * coil_maps.shape[1]) + coil_maps.shape[2:])


def encode(coils, slab_image, psf_values, pad_table):
    coil_count, lines, _, width = coils.shape
    readout = psf_values.shape[1]
    coil_image = complex_mul(coils.astype(jnp.float32), slab_image[None]).astype(jnp.bfloat16)
    spectra = jnp.dot(
        coil_image.reshape(coil_count * lines, 2 * width),
        pad_table,
        preferred_element_type=jnp.float32,
    )
    return turn_phase(spectra.reshape(coil_count, lines, 2, readout), psf_values[None]).astype(
        jnp.bfloat16
    )


def project(projector, waved):
    coil_count, lines, _, columns = waved.shape
    view_slices = waved.reshape(coil_count, lines // NY, NY, 2, columns)
    projected = jnp.einsum(
        "oaib,czbik->czaok", projector, view_slices, preferred_element_type=jnp.float32
    )
    return projected.astype(jnp.bfloat16).reshape(waved.shape)


def decode(coils, projected, psf_values, crop_table):
    coil_count, lines, _, readout = projected.shape
    width = coils.shape[3]
    unwaved = turn_phase(projected.astype(jnp.float32), -psf_values[None]).astype(jnp.bfloat16)
    back = jnp.dot(
        unwaved.reshape(coil_count * lines, 2 * readout),
        crop_table,
        preferred_element_type=jnp.float32,
    )
    return jnp.sum(
        conj_mul(coils.astype(jnp.float32), back.reshape(coil_count, lines, 2, width)), 0
    )


def round_up(size, step):
    return -(-size // step) * step


def host_dft(size_in, size_out, modulus):
    turns = np.outer(np.arange(size_in), np.arange(size_out)) % modulus
    angle = turns.astype(np.float64) * (2.0 * np.pi / modulus)
    factor = float(modulus) ** -0.5
    return np.cos(angle) * factor, np.sin(angle) * factor


def placed(table, rows, columns):
    out = np.zeros((rows, columns), np.float64)
    out[: table.shape[0], : table.shape[1]] = table
    return out


def split_table(table):
    high = table.astype(np.float32).astype(jnp.bfloat16)
    low = (table - high.astype(np.float64)).astype(np.float32).astype(jnp.bfloat16)
    return np.stack([high, low])


def host_tables(width, height, readout):
    tall = round_up(height, 256)
    cosine, sine = host_dft(readout, width, readout)
    encode_table = np.block([[cosine, sine], [-sine, cosine]])
    row_parts = host_dft(width, width, width)
    column_parts = [placed(part, tall, tall) for part in host_dft(height, height, height)]
    return (
        encode_table.astype(np.float32).astype(jnp.bfloat16),
        encode_table.T.astype(np.float32).astype(jnp.bfloat16),
        split_table(np.concatenate(row_parts, 0)),
        split_table(np.concatenate(column_parts, 1)),
    )


SINE = [(-1.0) ** n / math.factorial(2 * n + 1) for n in range(6)]
COSINE = [(-1.0) ** n / math.factorial(2 * n) for n in range(7)]


def poly(square, coefficients):
    value = jnp.full_like(square, coefficients[-1])
    for coefficient in reversed(coefficients[:-1]):
        value = value * square + coefficient
    return value


def cos_sin_of_half(half):
    square = half * half
    sine = half * poly(square, SINE)
    cosine = poly(square, COSINE)
    return 1.0 - 2.0 * sine * sine, 2.0 * sine * cosine


def cos_sin_turns(turns):
    rest = turns - jnp.floor(turns + 0.5)
    return cos_sin_of_half(rest * math.pi)


def split_value(value):
    high = value.astype(jnp.bfloat16)
    return high, (value - high.astype(jnp.float32)).astype(jnp.bfloat16)


def mxu(left, right):
    return jnp.dot(left, right, preferred_element_type=jnp.float32)


def slice_kernel(
    motion_ref,
    mask_ref,
    image_ref,
    psf_ref,
    row_ref,
    column_ref,
    coil_hbm,
    encode_hbm,
    decode_hbm,
    out_ref,
    coil_s,
    encode_s,
    decode_s,
    psf_s,
    mask_s,
    cosine_s,
    sine_s,
    phase_s,
    image_s,
    table_s,
    coil_image_s,
    waved_s,
    unwaved_s,
    sum_s,
    other_s,
    copy_sems,
):
    _, width, height = image_ref.shape
    readout = psf_ref.shape[1]
    tall = column_ref.shape[1]
    coils = coil_s.shape[0]

    copies = [
        pltpu.make_async_copy(source, target, copy_sems.at[at])
        for at, (source, target) in enumerate(
            [(coil_hbm, coil_s), (encode_hbm, encode_s), (decode_hbm, decode_s)]
        )
    ]
    for copy in copies:
        copy.start()
    partner = {"shot": 1 - lax.axis_index("shot")}
    barrier = pltpu.get_barrier_semaphore()
    pl.semaphore_signal(
        barrier, inc=1, device_id=partner, device_id_type=pl.DeviceIdType.MESH
    )

    psf_s[...] = jnp.zeros_like(psf_s)
    psf_s[:height, :readout] = psf_ref[...]
    turned_psf = jnp.transpose(psf_s[...])[:readout]
    turn_cosine, turn_sine = cos_sin_of_half(turned_psf * 0.5)
    cosine_s[...] = turn_cosine
    sine_s[...] = turn_sine

    theta = (motion_ref[0, 0].astype(jnp.float32) - (LEVELS - 1) / 2.0) * ANGLE_STEP
    shift_x = (motion_ref[0, 1].astype(jnp.float32) - (LEVELS - 1) / 2.0) * SHIFT_STEP
    shift_y = (motion_ref[0, 2].astype(jnp.float32) - (LEVELS - 1) / 2.0) * SHIFT_STEP
    half = theta * 0.5
    half_square = half * half
    slope = -half * (
        1.0
        + half_square
        * (1.0 / 3.0 + half_square * (2.0 / 15.0 + half_square * (17.0 / 315.0)))
    )
    square = theta * theta
    tilt = theta * (
        1.0 - square * (1.0 / 6.0 - square * (1.0 / 120.0 - square * (1.0 / 5040.0)))
    )

    place = lax.broadcasted_iota(jnp.int32, (width, tall), 0)
    line = lax.broadcasted_iota(jnp.int32, (width, tall), 1)
    across = line.astype(jnp.float32) - height / 2.0
    along = place.astype(jnp.float32) - width / 2.0
    place_freq = jnp.where(place < width // 2, place, place - width).astype(jnp.float32) / width
    line_freq = jnp.where(line < height // 2, line, line - height).astype(jnp.float32) / height
    for which, turns in enumerate(
        [
            (slope * across + shift_x) * place_freq,
            (tilt * along + shift_y) * line_freq,
            (slope * across) * place_freq,
        ]
    ):
        cosine, sine = cos_sin_turns(turns)
        phase_s[2 * which] = cosine
        phase_s[2 * which + 1] = sine

    def row_dft(real, imag):
        high, low = split_value(jnp.concatenate([real, imag], 1))
        table_high, table_low = row_ref[0], row_ref[1]
        out = mxu(table_high, high) + (mxu(table_high, low) + mxu(table_low, high))
        return (
            out[:width, :tall] + out[width:, tall:],
            out[:width, tall:] - out[width:, :tall],
        )

    def column_dft(real, imag):
        high, low = split_value(jnp.concatenate([real, imag], 0))
        table_high, table_low = column_ref[0], column_ref[1]
        out = mxu(high, table_high) + (mxu(low, table_high) + mxu(high, table_low))
        return (
            out[:width, :tall] + out[width:, tall:],
            out[width:, :tall] - out[:width, tall:],
        )

    def shear(dft, real, imag, which, sign):
        cosine = phase_s[2 * which]
        sine = phase_s[2 * which + 1]
        real, imag = dft(real, imag)
        turned = real * cosine + sign * (imag * sine)
        turned_negative = sign * (real * sine) - imag * cosine
        real, imag = dft(turned, turned_negative)
        return real, -imag

    image_s[...] = jnp.zeros_like(image_s)
    image_s[:, :, :height] = image_ref[...]
    real, imag = image_s[0], image_s[1]
    real, imag = shear(row_dft, real, imag, 0, 1.0)
    real, imag = shear(column_dft, real, imag, 1, 1.0)
    real, imag = shear(row_dft, real, imag, 2, 1.0)
    image_s[0] = real
    image_s[1] = imag

    mask_s[...] = jnp.zeros_like(mask_s)
    mask_s[:, :height] = mask_ref[...].astype(jnp.float32)
    weight = mask_s[...]

    def table_part(part, which):
        return column_ref[part, :, which * tall : (which + 1) * tall]

    def masked(part, which):
        return (table_part(part, which).astype(jnp.float32) * weight).astype(jnp.bfloat16)

    def triple(left, right):
        right_high, right_low = table_part(0, right), table_part(1, right)
        left_high, left_low = masked(0, left), masked(1, left)
        return mxu(left_high, right_high) + (
            mxu(left_low, right_high) + mxu(left_high, right_low)
        )

    table_real = triple(0, 0) + triple(1, 1)
    table_imag = triple(1, 0) - triple(0, 1)
    table_s[:tall, :tall] = table_real.astype(jnp.bfloat16)
    table_s[:tall, tall:] = (-table_imag).astype(jnp.bfloat16)
    table_s[tall:, :tall] = table_imag.astype(jnp.bfloat16)
    table_s[tall:, tall:] = table_real.astype(jnp.bfloat16)
    coil_image_s[...] = jnp.zeros_like(coil_image_s)
    sum_s[...] = jnp.zeros_like(sum_s)
    for copy in copies:
        copy.wait()

    pair = coil_image_s.shape[0]

    def some_coils(step, carry):
        for at in range(pair):
            coil = step * pair + at
            coil_real = coil_s[coil, 0].astype(jnp.float32)
            coil_imag = coil_s[coil, 1].astype(jnp.float32)
            real, imag = image_s[0, :, :height], image_s[1, :, :height]
            coil_image_s[at, :width, :height] = (coil_real * real - coil_imag * imag).astype(
                jnp.bfloat16
            )
            coil_image_s[at, width:, :height] = (coil_real * imag + coil_imag * real).astype(
                jnp.bfloat16
            )
        for at in range(pair):
            spectra = mxu(encode_s[...], coil_image_s[at])
            real, imag = spectra[:readout], spectra[readout:]
            cosine, sine = cosine_s[...], sine_s[...]
            waved_s[at, :, :tall] = (real * cosine - imag * sine).astype(jnp.bfloat16)
            waved_s[at, :, tall:] = (real * sine + imag * cosine).astype(jnp.bfloat16)
        for at in range(pair):
            projected = mxu(waved_s[at], table_s[...])
            real, imag = projected[:, :tall], projected[:, tall:]
            cosine, sine = cosine_s[...], sine_s[...]
            unwaved_s[at, :readout] = (real * cosine + imag * sine).astype(jnp.bfloat16)
            unwaved_s[at, readout:] = (imag * cosine - real * sine).astype(jnp.bfloat16)
        for at in range(pair):
            coil = step * pair + at
            back = mxu(decode_s[...], unwaved_s[at])
            real, imag = back[:width, :height], back[width:, :height]
            coil_real = coil_s[coil, 0].astype(jnp.float32)
            coil_imag = coil_s[coil, 1].astype(jnp.float32)
            sum_s[0, :, :height] += coil_real * real + coil_imag * imag
            sum_s[1, :, :height] += coil_real * imag - coil_imag * real
        return carry

    lax.fori_loop(0, coils // pair, some_coils, 0)

    real, imag = sum_s[0], sum_s[1]
    real, imag = shear(row_dft, real, imag, 2, -1.0)
    real, imag = shear(column_dft, real, imag, 1, -1.0)
    real, imag = shear(row_dft, real, imag, 0, -1.0)
    sum_s[0] = real
    sum_s[1] = imag
    pl.semaphore_wait(barrier, 1)
    copy = pltpu.make_async_remote_copy(
        src_ref=sum_s,
        dst_ref=other_s,
        send_sem=copy_sems.at[3],
        recv_sem=copy_sems.at[4],
        device_id=partner,
        device_id_type=pl.DeviceIdType.MESH,
    )
    copy.start()
    copy.wait()
    out_ref[...] = (sum_s[...] + other_s[...])[:, :, :height]


def whole_slice(image, coil_maps, psf_phase, line_mask, motion):
    height, width, readout = image.shape[0], image.shape[2], psf_phase.shape[1]
    coils = coil_maps.shape[0]
    tall = round_up(height, 256)
    pair = 2 if coils % 2 == 0 else 1
    planes = jnp.transpose(image, (1, 2, 0))
    coil_planes = jnp.transpose(coil_maps, (0, 2, 3, 1))
    encode_table, decode_table, row_table, column_table = [
        jnp.asarray(table) for table in host_tables(width, height, readout)
    ]
    vmem = pl.BlockSpec(memory_space=pltpu.VMEM)
    anywhere = pl.BlockSpec(memory_space=pl.ANY)
    total = pl.pallas_call(
        slice_kernel,
        out_shape=jax.ShapeDtypeStruct((2, width, height), jnp.float32),
        in_specs=[pl.BlockSpec(memory_space=pltpu.SMEM)] + [vmem] * 5 + [anywhere] * 3,
        out_specs=vmem,
        scratch_shapes=[
            pltpu.VMEM(coil_planes.shape, coil_planes.dtype),
            pltpu.VMEM(encode_table.shape, jnp.bfloat16),
            pltpu.VMEM(decode_table.shape, jnp.bfloat16),
            pltpu.VMEM((tall, round_up(readout, 128)), jnp.float32),
            pltpu.VMEM((1, tall), jnp.float32),
            pltpu.VMEM((readout, tall), jnp.float32),
            pltpu.VMEM((readout, tall), jnp.float32),
            pltpu.VMEM((6, width, tall), jnp.float32),
            pltpu.VMEM((2, width, tall), jnp.float32),
            pltpu.VMEM((2 * tall, 2 * tall), jnp.bfloat16),
            pltpu.VMEM((pair, 2 * width, tall), jnp.bfloat16),
            pltpu.VMEM((pair, readout, 2 * tall), jnp.bfloat16),
            pltpu.VMEM((pair, 2 * readout, tall), jnp.bfloat16),
            pltpu.VMEM((2, width, tall), jnp.float32),
            pltpu.VMEM((2, width, tall), jnp.float32),
            pltpu.SemaphoreType.DMA((5,)),
        ],
        compiler_params=pltpu.CompilerParams(
            vmem_limit_bytes=56 * 1024 * 1024, collective_id=0, has_side_effects=True
        ),
        name="slice_kernel",
    )(
        motion,
        line_mask,
        planes,
        psf_phase,
        row_table,
        column_table,
        coil_planes,
        encode_table,
        decode_table,
    )
    return jnp.transpose(total, (2, 0, 1))


def on_device(image, coil_maps, psf_phase, line_mask, motion):
    lines = image.shape[0]
    width = image.shape[2]
    readout = psf_phase.shape[1]
    if lines == NY and lax.axis_size("shot") == 2:
        return whole_slice(image, coil_maps, psf_phase, line_mask, motion)
    devices = lax.axis_size("space")
    device_rank = lax.axis_index("space")
    pad_table = block(dft_parts(width, readout, readout, -1.0)).astype(jnp.bfloat16)
    crop_table = block(dft_parts(readout, width, readout, 1.0)).astype(jnp.bfloat16)
    group_size = max(1, NY // lines)
    bit_count = group_size.bit_length() - 1
    own_coils = regroup_coils(coil_maps, bit_count, device_rank)
    own_psf = gather_slice(psf_phase, bit_count, device_rank)
    projector = line_table(line_mask[0])
    rotated = rotate_shards(image, motion[0], 1, device_rank, devices)
    slab_image = gather_slice(rotated, bit_count, device_rank)
    waved = encode(own_coils, slab_image, own_psf, pad_table)
    partial_sum = decode(own_coils, project(projector, waved), own_psf, crop_table)
    combined = sum_slice(partial_sum, bit_count, device_rank)
    running = rotate_shards(combined, motion[0], -1, device_rank, devices)
    return lax.psum(running, "shot")


def solution(mesh):
    in_specs = (
        P(("parts", "space"), None, None),
        P(None, ("parts", "space"), None, None),
        P(("parts", "space"), None),
        P(("parts", "shot"), None),
        P(("parts", "shot"), None),
    )
    out_specs = P(("parts", "space"), None, None)
    return jax.shard_map(
        on_device, mesh=mesh, in_specs=in_specs, out_specs=out_specs, check_vma=False
    )
```

profile of v0, /device:TPU:9, one launch (start us, length us, event | category | flops | bytes accessed | tf_op | source)
XLA Modules:
  0.0 34.2 jit_solution(2277806432569306486)
XLA Ops:
  0.0 32.5 %slice_kernel.1 = f32[2,192,200]{2,1,0:T(8,128)} custom-call(s32[1,3]{1,0:T(1,128)} %motion_ref.1, s32[1,200]{1,0:T(1,128)} %mask_ref.1, f32[2,192,200]{2,1,0:T(8,128)} %bitcast.5, f32[200,576]{1,0:T(8,128)} %psf_ref.1, bf16[2,384,192]{2,1,0:T(8,128)(2,1)} %constant.10.clone.row_ref, bf16[2,256,512]{2,1,0:T(8,128)(2,1)} %constant.11.clone.column_ref, ...), custom_call_target="tpu_custom_call" | custom-call | tf_op jit(solution)/shard_map/slice_kernel/pallas_call | solution.py:534
  32.5 1.8 %copy.11 = f32[200,2,192]{0,2,1:T(8,128)} copy(f32[200,2,192]{0,2,1:T(8,128)} %bitcast.4) | data formatting | bytes 614400
where the time goes:
time: 34.4 us; the launch traced here: 34.2 us
  Pallas kernels  32.5 us (94%)
  local copies, waits for them, and re-layouts  1.77 us (5%)
    pallas_call x1, Pallas kernels, whole_slice(): pl.pallas_call(slice_kernel, out_shape=jax.ShapeDtypeStruct((2, width, he...  32.5 us
    unnamed x1, local copies, waits for them, and re-layouts  1.77 us

commit v1 on v0

--- a/solution.py
+++ b/solution.py
@@ -246,17 +246,32 @@
     return -(-size // step) * step
 
 
-def host_dft(size_in, size_out, modulus):
-    turns = np.outer(np.arange(size_in), np.arange(size_out)) % modulus
+HALF = 128
+TALL = 2 * HALF
+
+
+def fits(height, width, readout):
+    return (
+        height % 2 == 0
+        and HALF < height
+        and height // 2 < HALF
+        and width % 32 == 0
+        and width <= TALL
+        and readout % 32 == 0
+    )
+
+
+def cosine_sine(rows, columns, modulus):
+    turns = np.outer(rows, columns) % modulus
     angle = turns.astype(np.float64) * (2.0 * np.pi / modulus)
-    factor = float(modulus) ** -0.5
-    return np.cos(angle) * factor, np.sin(angle) * factor
-
-
-def placed(table, rows, columns):
-    out = np.zeros((rows, columns), np.float64)
-    out[: table.shape[0], : table.shape[1]] = table
-    return out
+    return np.cos(angle), np.sin(angle)
+
+
+def half_spectrum(points, modulus):
+    half = modulus // 2
+    cosine, sine = cosine_sine(np.arange(half), points, modulus)
+    sine[0] = cosine_sine([half], points, modulus)[0][0]
+    return np.concatenate([cosine, sine], 0)
 
 
 def split_table(table):
@@ -266,16 +281,56 @@
 
 
 def host_tables(width, height, readout):
-    tall = round_up(height, 256)
-    cosine, sine = host_dft(readout, width, readout)
-    encode_table = np.block([[cosine, sine], [-sine, cosine]])
-    row_parts = host_dft(width, width, width)
-    column_parts = [placed(part, tall, tall) for part in host_dft(height, height, height)]
-    return (
-        encode_table.astype(np.float32).astype(jnp.bfloat16),
-        encode_table.T.astype(np.float32).astype(jnp.bfloat16),
-        split_table(np.concatenate(row_parts, 0)),
-        split_table(np.concatenate(column_parts, 1)),
+    spectrum = half_spectrum(np.arange(width), readout) * readout**-0.5
+    weight = np.full((width, 1), (2.0 / width) ** 0.5)
+    weight[0] = weight[width // 2] = width**-0.5
+    row = half_spectrum(np.arange(width), width) * weight
+
+    middle = height // 2
+    lines = np.arange(height)
+    spread = np.where(lines < middle, lines, lines - middle + HALF)
+    cosine, sine = cosine_sine(lines, np.arange(middle + 1), height)
+    wave = np.zeros((height, TALL))
+    wave[:, : middle + 1] = cosine * (2.0 / height) ** 0.5
+    wave[:, 0] = height**-0.5
+    wave[:, middle] = cosine[:, middle] * height**-0.5
+    wave[:, HALF + 1 : HALF + middle] = sine[:, 1:middle] * (2.0 / height) ** 0.5
+    natural = np.zeros((TALL, TALL))
+    natural[:height] = wave
+    padded = np.zeros((TALL, TALL))
+    padded[spread] = wave
+
+    cosine, sine = [part * height**-0.5 for part in cosine_sine(lines, lines, height)]
+    line_left = np.zeros((HALF, 2 * TALL))
+    line_left[:middle, :height] = cosine[:middle]
+    line_left[:middle, TALL : TALL + height] = sine[:middle]
+    line_right = np.zeros((2 * TALL, TALL))
+    line_right[:height, :middle] = cosine[:, :middle]
+    line_right[TALL : TALL + height, :middle] = sine[:, :middle]
+    line_right[:height, HALF : HALF + middle] = sine[:, :middle]
+    line_right[TALL : TALL + height, HALF : HALF + middle] = -cosine[:, :middle]
+
+    spreader = np.zeros((TALL, TALL))
+    spreader[lines, spread] = 1.0
+    mirror = np.zeros((readout // 2, readout // 2))
+    mirror[np.arange(readout // 2), -np.arange(readout // 2) % (readout // 2)] = 1.0
+
+    def narrow(table):
+        return table.astype(np.float32).astype(jnp.bfloat16)
+
+    return dict(
+        row=split_table(row),
+        row_back=split_table(row.T),
+        column=split_table(natural),
+        column_spread_back=split_table(padded.T),
+        column_spread=split_table(padded),
+        column_back=split_table(natural.T),
+        spreader=narrow(spreader),
+        mirror=narrow(mirror),
+        line_left=split_table(line_left),
+        line_right=split_table(line_right),
+        encode=narrow(spectrum),
+        decode=narrow(spectrum.T),
     )
 
 
@@ -311,59 +366,74 @@
     return jnp.dot(left, right, preferred_element_type=jnp.float32)
 
 
-def slice_kernel(
-    motion_ref,
-    mask_ref,
-    image_ref,
-    psf_ref,
-    row_ref,
-    column_ref,
-    coil_hbm,
-    encode_hbm,
-    decode_hbm,
-    out_ref,
-    coil_s,
-    encode_s,
-    decode_s,
-    psf_s,
-    mask_s,
-    cosine_s,
-    sine_s,
-    phase_s,
-    image_s,
-    table_s,
-    coil_image_s,
-    waved_s,
-    unwaved_s,
-    sum_s,
-    other_s,
-    copy_sems,
-):
-    _, width, height = image_ref.shape
-    readout = psf_ref.shape[1]
-    tall = column_ref.shape[1]
-    coils = coil_s.shape[0]
-
-    copies = [
-        pltpu.make_async_copy(source, target, copy_sems.at[at])
-        for at, (source, target) in enumerate(
-            [(coil_hbm, coil_s), (encode_hbm, encode_s), (decode_hbm, decode_s)]
-        )
-    ]
-    for copy in copies:
-        copy.start()
+def mxu_split(left, right):
+    return mxu(left[0], right[0]) + (mxu(left[0], right[1]) + mxu(left[1], right[0]))
+
+
+LOADS = (
+    "image",
+    "row",
+    "row_back",
+    "psf",
+    "column",
+    "column_spread_back",
+    "spreader",
+    "mirror",
+    "line_left",
+    "line_right",
+    "coil",
+    "encode",
+    "decode",
+    "column_spread",
+    "column_back",
+)
+UNROLL = 4
+SPLIT = 2
+
+
+def slice_kernel(motion_ref, mask_ref, *refs):
+    count = len(LOADS)
+    sources = dict(zip(LOADS, refs[:count]))
+    out_ref = refs[count]
+    held = dict(zip(LOADS, refs[count + 1 : 2 * count + 1]))
+    (
+        image_s,
+        psf_s,
+        tail_s,
+        coil_s,
+        mask_s,
+        table_s,
+        turn_s,
+        row_phase_s,
+        edge_phase_s,
+        column_phase_s,
+        rotated_s,
+        coil_image_s,
+        fold_s,
+        unwaved_s,
+        sum_s,
+        other_s,
+        load_sems,
+        link_sems,
+    ) = refs[2 * count + 1 :]
+    _, width, height = sources["image"].shape
+    readout = sources["psf"].shape[0]
+    coils = sources["coil"].shape[0]
+    half_width, half_readout = width // 2, readout // 2
+    tail = height - HALF
+    ahead = HALF - height // 2
+
+    copies = {
+        name: pltpu.make_async_copy(sources[name], held[name], load_sems.at[at])
+        for at, name in enumerate(LOADS)
+    }
+    for name in LOADS:
+        copies[name].start()
     partner = {"shot": 1 - lax.axis_index("shot")}
     barrier = pltpu.get_barrier_semaphore()
     pl.semaphore_signal(
         barrier, inc=1, device_id=partner, device_id_type=pl.DeviceIdType.MESH
     )
-
-    psf_s[...] = jnp.zeros_like(psf_s)
-    psf_s[:height, :readout] = psf_ref[...]
-    turned_psf = jnp.transpose(psf_s[...])[:readout]
-    turn_cosine, turn_sine = cos_sin_of_half(turned_psf * 0.5)
-    cosine_s[...] = turn_cosine
-    sine_s[...] = turn_sine
 
     theta = (motion_ref[0, 0].astype(jnp.float32) - (LEVELS - 1) / 2.0) * ANGLE_STEP
     shift_x = (motion_ref[0, 1].astype(jnp.float32) - (LEVELS - 1) / 2.0) * SHIFT_STEP
@@ -380,195 +450,334 @@
         1.0 - square * (1.0 / 6.0 - square * (1.0 / 120.0 - square * (1.0 / 5040.0)))
     )
 
-    place = lax.broadcasted_iota(jnp.int32, (width, tall), 0)
-    line = lax.broadcasted_iota(jnp.int32, (width, tall), 1)
-    across = line.astype(jnp.float32) - height / 2.0
-    along = place.astype(jnp.float32) - width / 2.0
-    place_freq = jnp.where(place < width // 2, place, place - width).astype(jnp.float32) / width
-    line_freq = jnp.where(line < height // 2, line, line - height).astype(jnp.float32) / height
-    for which, turns in enumerate(
-        [
-            (slope * across + shift_x) * place_freq,
-            (tilt * along + shift_y) * line_freq,
-            (slope * across) * place_freq,
+    def iota(shape, axis):
+        return lax.broadcasted_iota(jnp.int32, shape, axis)
+
+    def floats(value):
+        return value.astype(jnp.float32)
+
+    def row_phase(slot, padded, shift):
+        lane = iota((8, TALL), 1)
+        line = jnp.where(lane < HALF, lane, lane - ahead) if padded else lane
+        distance = slope * (floats(line) - height / 2.0) + shift
+        row = iota((8, TALL), 0)
+        edge = distance * jnp.where(row == 0, 0.5, floats(row) * (1.0 / width))
+        edge_phase_s[slot, 0], edge_phase_s[slot, 1] = cos_sin_turns(edge)
+        for at in range(0, half_width, 8):
+            turns = distance * (floats(row + at) * (1.0 / width))
+            cosine, sine = cos_sin_turns(turns)
+            row_phase_s[slot, 0, at : at + 8] = cosine
+            row_phase_s[slot, 1, at : at + 8] = sine
+
+    def column_phase():
+        frequency = floats(iota((16, HALF), 1)) * (1.0 / height)
+        row = iota((16, HALF), 0)
+        for at in range(0, width, 16):
+            turns = (tilt * (floats(row + at) - width / 2.0) + shift_y) * frequency
+            cosine, sine = cos_sin_turns(turns)
+            column_phase_s[0, at : at + 16] = cosine
+            column_phase_s[1, at : at + 16] = sine
+
+    def rows_of(table, part, span):
+        return held[table][part] if span is None else held[table][part, span[0] : span[1]]
+
+    def row_apply(table, value, span=None):
+        return mxu_split((rows_of(table, 0, span), rows_of(table, 1, span)), value)
+
+    def column_apply(table, value):
+        return mxu_split(split_value(value), (held[table][0], held[table][1]))
+
+    def turn_rows(real, imag, slot, sign):
+        cosine, sine = row_phase_s[slot, 0], sign * row_phase_s[slot, 1]
+        edge_cosine, edge_sine = edge_phase_s[slot, 0], sign * edge_phase_s[slot, 1]
+        real = row_apply("row", split_value(real))
+        imag = row_apply("row", split_value(imag))
+        first = iota((8, TALL), 0) == 0
+        even = [value[:half_width] for value in (real, imag)]
+        odd = [value[half_width:] for value in (real, imag)]
+        mixed = [
+            jnp.where(first, -odd[1][:8], even[0][:8]),
+            jnp.where(first, odd[0][:8], even[1][:8]),
         ]
-    ):
-        cosine, sine = cos_sin_turns(turns)
-        phase_s[2 * which] = cosine
-        phase_s[2 * which + 1] = sine
-
-    def row_dft(real, imag):
-        high, low = split_value(jnp.concatenate([real, imag], 1))
-        table_high, table_low = row_ref[0], row_ref[1]
-        out = mxu(table_high, high) + (mxu(table_high, low) + mxu(table_low, high))
-        return (
-            out[:width, :tall] + out[width:, tall:],
-            out[:width, tall:] - out[width:, :tall],
+        return [
+            split_value(
+                jnp.concatenate(
+                    [
+                        cosine * even[at] - sine * odd[at],
+                        edge_sine * mixed[at] + edge_cosine * odd[at][:8],
+                        sine[8:] * even[at][8:] + cosine[8:] * odd[at][8:],
+                    ],
+                    0,
+                )
+            )
+            for at in range(2)
+        ]
+
+    def shear_rows(real, imag, slot, sign):
+        real, imag = turn_rows(real, imag, slot, sign)
+        return row_apply("row_back", real), row_apply("row_back", imag)
+
+    def shear_columns(real, imag, tables, sign):
+        cosine, sine = column_phase_s[0], sign * column_phase_s[1]
+        real, imag = column_apply(tables[0], real), column_apply(tables[0], imag)
+        even = [value[:, :HALF] for value in (real, imag)]
+        odd = [value[:, HALF:] for value in (real, imag)]
+        last = iota((width, HALF), 1) == height // 2
+        mixed = [jnp.where(last, even[1], odd[0]), jnp.where(last, -even[0], odd[1])]
+        out = []
+        for at in range(2):
+            out.append(
+                jnp.concatenate(
+                    [
+                        cosine * even[at] - sine * mixed[at],
+                        sine * even[at] + cosine * odd[at],
+                    ],
+                    1,
+                )
+            )
+        return column_apply(tables[1], out[0]), column_apply(tables[1], out[1])
+
+    image_s[...] = jnp.zeros_like(image_s)
+    psf_s[:, HALF:] = jnp.zeros((readout, TALL - HALF), jnp.float32)
+    tail_s[...] = jnp.zeros_like(tail_s)
+    mask_s[...] = jnp.zeros_like(mask_s)
+    mask_s[:, :height] = floats(mask_ref[...])
+    row_phase(0, False, shift_x)
+    column_phase()
+    row_phase(1, True, 0.0)
+    copies["image"].wait()
+    copies["row"].wait()
+    copies["row_back"].wait()
+    image_s[:, :, :height] = held["image"][...]
+    real, imag = shear_rows(image_s[0], image_s[1], 0, 1.0)
+    copies["column"].wait()
+    copies["column_spread_back"].wait()
+    real, imag = shear_columns(real, imag, ("column", "column_spread_back"), 1.0)
+
+    copies["psf"].wait()
+    psf_s[:, :height] = held["psf"][...]
+    copies["spreader"].wait()
+    copies["mirror"].wait()
+    for at in range(0, readout, 32):
+        turn = cos_sin_of_half(psf_s[at : at + 32] * 0.5)
+        for which in range(2):
+            value = mxu(turn[which].astype(jnp.bfloat16), held["spreader"][...])
+            value = value.astype(jnp.bfloat16)
+            for part in range(2):
+                turn_s[which, part, at : at + 32] = value[:, part * HALF : (part + 1) * HALF]
+    behind = jnp.concatenate(
+        [turn_s[which, part, half_readout:] for which in range(2) for part in range(2)], 1
+    )
+    behind = mxu(held["mirror"][...], behind).astype(jnp.bfloat16)
+    for at in range(4):
+        turn_s[at // 2, at % 2, half_readout:] = behind[:, at * HALF : (at + 1) * HALF]
+
+    copies["line_left"].wait()
+    copies["line_right"].wait()
+    mask = mask_s[...]
+    mask = jnp.concatenate([mask, mask], 1)
+    odd_line = iota(mask.shape, 1) % 2
+    for parity in range(2):
+        chosen = jnp.where(odd_line == parity, mask, 0.0)
+        left = [
+            (floats(held["line_left"][part]) * chosen).astype(jnp.bfloat16) for part in range(2)
+        ]
+        table = mxu_split(left, (held["line_right"][0], held["line_right"][1]))
+        direct, crossed = table[:, :HALF], table[:, HALF:]
+        table_s[parity, :HALF] = table.astype(jnp.bfloat16)
+        table_s[parity, HALF:, :HALF] = (-crossed).astype(jnp.bfloat16)
+        table_s[parity, HALF:, HALF:] = direct.astype(jnp.bfloat16)
+
+    real, imag = shear_rows(real, imag, 1, 1.0)
+    for part in range(2):
+        rotated_s[part, 0] = real[:, part * HALF : (part + 1) * HALF]
+        rotated_s[part, 1] = imag[:, part * HALF : (part + 1) * HALF]
+    sum_s[...] = jnp.zeros_like(sum_s)
+
+    copies["coil"].wait()
+    copies["encode"].wait()
+    copies["decode"].wait()
+
+    def multiply(coil, slot):
+        early = iota((width, HALF), 1) < ahead
+        spread = []
+        for at in range(2):
+            low = floats(held["coil"][coil, at, :, :HALF])
+            tail_s[at, :, :tail] = floats(held["coil"][coil, at, :, HALF:height])
+            high = jnp.where(
+                early, pltpu.roll(low, ahead, 1), pltpu.roll(tail_s[at], ahead, 1)
+            )
+            spread.append((low, high))
+            coil_s[slot, at, 0] = low
+            coil_s[slot, at, 1] = high
+        for part in range(2):
+            real, imag = rotated_s[part, 0], rotated_s[part, 1]
+            coil_real, coil_imag = spread[0][part], spread[1][part]
+            coil_image_s[part] = (coil_real * real - coil_imag * imag).astype(jnp.bfloat16)
+            coil_image_s[2 + part] = (coil_real * imag + coil_imag * real).astype(jnp.bfloat16)
+
+    def head(value):
+        return value[:16]
+
+    first = iota((16, HALF), 0) == 0
+
+    def joined(chosen, value):
+        return jnp.concatenate([jnp.where(first, chosen[:16], value[:16]), value[16:]], 0)
+
+    def encode():
+        spectra = mxu(
+            held["encode"][...], jnp.concatenate([coil_image_s[at] for at in range(4)], 1)
         )
-
-    def column_dft(real, imag):
-        high, low = split_value(jnp.concatenate([real, imag], 0))
-        table_high, table_low = column_ref[0], column_ref[1]
-        out = mxu(high, table_high) + (mxu(low, table_high) + mxu(high, table_low))
-        return (
-            out[:width, :tall] + out[width:, tall:],
-            out[width:, :tall] - out[:width, tall:],
+        waved = []
+        for part in range(2):
+            lanes = slice(part * HALF, (part + 1) * HALF)
+            even_real, even_imag = spectra[:half_readout, :TALL], spectra[:half_readout, TALL:]
+            odd_real, odd_imag = spectra[half_readout:, :TALL], spectra[half_readout:, TALL:]
+            even_real, even_imag = even_real[:, lanes], even_imag[:, lanes]
+            odd_real, odd_imag = odd_real[:, lanes], odd_imag[:, lanes]
+            sides = (
+                (joined(even_real, even_real + odd_imag), joined(even_imag, even_imag - odd_real)),
+                (joined(odd_real, even_real - odd_imag), joined(odd_imag, even_imag + odd_real)),
+            )
+            for side, (real, imag) in enumerate(sides):
+                real, imag = real.astype(jnp.bfloat16), imag.astype(jnp.bfloat16)
+                rows = slice(side * half_readout, (side + 1) * half_readout)
+                cosine, sine = turn_s[0, part, rows], turn_s[1, part, rows]
+                waved.append((real * cosine - imag * sine, real * sine + imag * cosine))
+        for side in range(2):
+            rows = slice(side * half_readout, (side + 1) * half_readout)
+            for at in range(2):
+                low, high = waved[side][at], waved[2 + side][at]
+                fold_s[0, at, rows] = low + high
+                fold_s[1, at, rows] = low - high
+
+    def project():
+        even, odd = [
+            mxu(jnp.concatenate([fold_s[at, 0], fold_s[at, 1]], 1), table_s[at])
+            for at in range(2)
+        ]
+        for part, value in enumerate((even + odd, even - odd)):
+            value = value.astype(jnp.bfloat16)
+            real, imag = value[:, :HALF], value[:, HALF:]
+            cosine, sine = turn_s[0, part], turn_s[1, part]
+            unreal, unimag = real * cosine + imag * sine, imag * cosine - real * sine
+            plus_real, minus_real = unreal[:half_readout], unreal[half_readout:]
+            plus_imag, minus_imag = unimag[:half_readout], unimag[half_readout:]
+            unwaved_s[part, :half_readout] = joined(plus_real, plus_real + minus_real)
+            unwaved_s[2 + part, :half_readout] = joined(plus_imag, plus_imag + minus_imag)
+            unwaved_s[part, half_readout:] = joined(minus_real, minus_imag - plus_imag)
+            unwaved_s[2 + part, half_readout:] = joined(minus_imag, plus_real - minus_real)
+
+    def decode(slot):
+        back = mxu(held["decode"][...], jnp.concatenate([unwaved_s[at] for at in range(4)], 1))
+        for part in range(2):
+            real = back[:, part * HALF : (part + 1) * HALF]
+            imag = back[:, TALL + part * HALF : TALL + (part + 1) * HALF]
+            coil_real, coil_imag = coil_s[slot, 0, part], coil_s[slot, 1, part]
+            sum_s[0, part] += coil_real * real + coil_imag * imag
+            sum_s[1, part] += coil_real * imag - coil_imag * real
+
+    multiply(0, 0)
+    encode()
+    multiply(1, 1)
+    project()
+    encode()
+    multiply(2, 2)
+
+    def step(at, carry):
+        for inner in range(UNROLL):
+            decode(inner)
+            project()
+            encode()
+            multiply(at * UNROLL + inner + 3, (inner + 3) % UNROLL)
+        return carry
+
+    rounds = (coils - 3) // UNROLL
+    lax.fori_loop(0, rounds, step, 0)
+    for coil in range(rounds * UNROLL, coils):
+        decode(coil % UNROLL)
+        if coil + 1 < coils:
+            project()
+        if coil + 2 < coils:
+            encode()
+        if coil + 3 < coils:
+            multiply(coil + 3, (coil + 3) % UNROLL)
+
+    copies["column_spread"].wait()
+    copies["column_back"].wait()
+    real, imag = [jnp.concatenate([sum_s[at, 0], sum_s[at, 1]], 1) for at in range(2)]
+    real, imag = shear_rows(real, imag, 1, -1.0)
+    real, imag = shear_columns(real, imag, ("column_spread", "column_back"), -1.0)
+    halves = turn_rows(real, imag, 0, -1.0)
+    pl.semaphore_wait(barrier, 1)
+    size = width // SPLIT
+    links = []
+    for at in range(SPLIT):
+        span = (at * size, (at + 1) * size)
+        for part in range(2):
+            image_s[part, span[0] : span[1]] = row_apply("row_back", halves[part], span)
+        links.append(
+            pltpu.make_async_remote_copy(
+                src_ref=image_s.at[:, pl.ds(span[0], size)],
+                dst_ref=other_s.at[:, pl.ds(span[0], size)],
+                send_sem=link_sems.at[2 * at],
+                recv_sem=link_sems.at[2 * at + 1],
+                device_id=partner,
+                device_id_type=pl.DeviceIdType.MESH,
+            )
         )
-
-    def shear(dft, real, imag, which, sign):
-        cosine = phase_s[2 * which]
-        sine = phase_s[2 * which + 1]
-        real, imag = dft(real, imag)
-        turned = real * cosine + sign * (imag * sine)
-        turned_negative = sign * (real * sine) - imag * cosine
-        real, imag = dft(turned, turned_negative)
-        return real, -imag
-
-    image_s[...] = jnp.zeros_like(image_s)
-    image_s[:, :, :height] = image_ref[...]
-    real, imag = image_s[0], image_s[1]
-    real, imag = shear(row_dft, real, imag, 0, 1.0)
-    real, imag = shear(column_dft, real, imag, 1, 1.0)
-    real, imag = shear(row_dft, real, imag, 2, 1.0)
-    image_s[0] = real
-    image_s[1] = imag
-
-    mask_s[...] = jnp.zeros_like(mask_s)
-    mask_s[:, :height] = mask_ref[...].astype(jnp.float32)
-    weight = mask_s[...]
-
-    def table_part(part, which):
-        return column_ref[part, :, which * tall : (which + 1) * tall]
-
-    def masked(part, which):
-        return (table_part(part, which).astype(jnp.float32) * weight).astype(jnp.bfloat16)
-
-    def triple(left, right):
-        right_high, right_low = table_part(0, right), table_part(1, right)
-        left_high, left_low = masked(0, left), masked(1, left)
-        return mxu(left_high, right_high) + (
-            mxu(left_low, right_high) + mxu(left_high, right_low)
-        )
-
-    table_real = triple(0, 0) + triple(1, 1)
-    table_imag = triple(1, 0) - triple(0, 1)
-    table_s[:tall, :tall] = table_real.astype(jnp.bfloat16)
-    table_s[:tall, tall:] = (-table_imag).astype(jnp.bfloat16)
-    table_s[tall:, :tall] = table_imag.astype(jnp.bfloat16)
-    table_s[tall:, tall:] = table_real.astype(jnp.bfloat16)
-    coil_image_s[...] = jnp.zeros_like(coil_image_s)
-    sum_s[...] = jnp.zeros_like(sum_s)
-    for copy in copies:
-        copy.wait()
-
-    pair = coil_image_s.shape[0]
-
-    def some_coils(step, carry):
-        for at in range(pair):
-            coil = step * pair + at
-            coil_real = coil_s[coil, 0].astype(jnp.float32)
-            coil_imag = coil_s[coil, 1].astype(jnp.float32)
-            real, imag = image_s[0, :, :height], image_s[1, :, :height]
-            coil_image_s[at, :width, :height] = (coil_real * real - coil_imag * imag).astype(
-                jnp.bfloat16
-            )
-            coil_image_s[at, width:, :height] = (coil_real * imag + coil_imag * real).astype(
-                jnp.bfloat16
-            )
-        for at in range(pair):
-            spectra = mxu(encode_s[...], coil_image_s[at])
-            real, imag = spectra[:readout], spectra[readout:]
-            cosine, sine = cosine_s[...], sine_s[...]
-            waved_s[at, :, :tall] = (real * cosine - imag * sine).astype(jnp.bfloat16)
-            waved_s[at, :, tall:] = (real * sine + imag * cosine).astype(jnp.bfloat16)
-        for at in range(pair):
-            projected = mxu(waved_s[at], table_s[...])
-            real, imag = projected[:, :tall], projected[:, tall:]
-            cosine, sine = cosine_s[...], sine_s[...]
-            unwaved_s[at, :readout] = (real * cosine + imag * sine).astype(jnp.bfloat16)
-            unwaved_s[at, readout:] = (imag * cosine - real * sine).astype(jnp.bfloat16)
-        for at in range(pair):
-            coil = step * pair + at
-            back = mxu(decode_s[...], unwaved_s[at])
-            real, imag = back[:width, :height], back[width:, :height]
-            coil_real = coil_s[coil, 0].astype(jnp.float32)
-            coil_imag = coil_s[coil, 1].astype(jnp.float32)
-            sum_s[0, :, :height] += coil_real * real + coil_imag * imag
-            sum_s[1, :, :height] += coil_real * imag - coil_imag * real
-        return carry
-
-    lax.fori_loop(0, coils // pair, some_coils, 0)
-
-    real, imag = sum_s[0], sum_s[1]
-    real, imag = shear(row_dft, real, imag, 2, -1.0)
-    real, imag = shear(column_dft, real, imag, 1, -1.0)
-    real, imag = shear(row_dft, real, imag, 0, -1.0)
-    sum_s[0] = real
-    sum_s[1] = imag
-    pl.semaphore_wait(barrier, 1)
-    copy = pltpu.make_async_remote_copy(
-        src_ref=sum_s,
-        dst_ref=other_s,
-        send_sem=copy_sems.at[3],
-        recv_sem=copy_sems.at[4],
-        device_id=partner,
-        device_id_type=pl.DeviceIdType.MESH,
-    )
-    copy.start()
-    copy.wait()
-    out_ref[...] = (sum_s[...] + other_s[...])[:, :, :height]
+        links[at].start()
+    for at in range(SPLIT):
+        links[at].wait_recv()
+        rows = slice(at * size, (at + 1) * size)
+        out_ref[:, rows] = (image_s[:, rows] + other_s[:, rows])[:, :, :height]
+    for at in range(SPLIT):
+        links[at].wait_send()
 
 
 def whole_slice(image, coil_maps, psf_phase, line_mask, motion):
     height, width, readout = image.shape[0], image.shape[2], psf_phase.shape[1]
     coils = coil_maps.shape[0]
-    tall = round_up(height, 256)
-    pair = 2 if coils % 2 == 0 else 1
-    planes = jnp.transpose(image, (1, 2, 0))
-    coil_planes = jnp.transpose(coil_maps, (0, 2, 3, 1))
-    encode_table, decode_table, row_table, column_table = [
-        jnp.asarray(table) for table in host_tables(width, height, readout)
-    ]
+    arrays = {
+        name: jnp.asarray(table) for name, table in host_tables(width, height, readout).items()
+    }
+    arrays["image"] = jnp.transpose(image, (1, 2, 0))
+    arrays["coil"] = jnp.transpose(coil_maps, (0, 2, 3, 1))
+    arrays["psf"] = jnp.transpose(psf_phase)
+    loads = [arrays[name] for name in LOADS]
     vmem = pl.BlockSpec(memory_space=pltpu.VMEM)
     anywhere = pl.BlockSpec(memory_space=pl.ANY)
     total = pl.pallas_call(
         slice_kernel,
         out_shape=jax.ShapeDtypeStruct((2, width, height), jnp.float32),
-        in_specs=[pl.BlockSpec(memory_space=pltpu.SMEM)] + [vmem] * 5 + [anywhere] * 3,
+        in_specs=[pl.BlockSpec(memory_space=pltpu.SMEM), vmem] + [anywhere] * len(LOADS),
         out_specs=vmem,
-        scratch_shapes=[
-            pltpu.VMEM(coil_planes.shape, coil_planes.dtype),
-            pltpu.VMEM(encode_table.shape, jnp.bfloat16),
-            pltpu.VMEM(decode_table.shape, jnp.bfloat16),
-            pltpu.VMEM((tall, round_up(readout, 128)), jnp.float32),
-            pltpu.VMEM((1, tall), jnp.float32),
-            pltpu.VMEM((readout, tall), jnp.float32),
-            pltpu.VMEM((readout, tall), jnp.float32),
-            pltpu.VMEM((6, width, tall), jnp.float32),
-            pltpu.VMEM((2, width, tall), jnp.float32),
-            pltpu.VMEM((2 * tall, 2 * tall), jnp.bfloat16),
-            pltpu.VMEM((pair, 2 * width, tall), jnp.bfloat16),
-            pltpu.VMEM((pair, readout, 2 * tall), jnp.bfloat16),
-            pltpu.VMEM((pair, 2 * readout, tall), jnp.bfloat16),
-            pltpu.VMEM((2, width, tall), jnp.float32),
-            pltpu.VMEM((2, width, tall), jnp.float32),
-            pltpu.SemaphoreType.DMA((5,)),
+        scratch_shapes=[pltpu.VMEM(value.shape, value.dtype) for value in loads]
+        + [
+            pltpu.VMEM((2, width, TALL), jnp.float32),
+            pltpu.VMEM((readout, TALL), jnp.float32),
+            pltpu.VMEM((2, width, HALF), jnp.float32),
+            pltpu.VMEM((UNROLL, 2, 2, width, HALF), jnp.float32),
+            pltpu.VMEM((1, TALL), jnp.float32),
+            pltpu.VMEM((2, TALL, TALL), jnp.bfloat16),
+            pltpu.VMEM((2, 2, readout, HALF), jnp.bfloat16),
+            pltpu.VMEM((2, 2, width // 2, TALL), jnp.float32),
+            pltpu.VMEM((2, 2, 8, TALL), jnp.float32),
+            pltpu.VMEM((2, width, HALF), jnp.float32),
+            pltpu.VMEM((2, 2, width, HALF), jnp.float32),
+            pltpu.VMEM((4, width, HALF), jnp.bfloat16),
+            pltpu.VMEM((2, 2, readout, HALF), jnp.bfloat16),
+            pltpu.VMEM((4, readout, HALF), jnp.bfloat16),
+            pltpu.VMEM((2, 2, width, HALF), jnp.float32),
+            pltpu.VMEM((2, width, TALL), jnp.float32),
+            pltpu.SemaphoreType.DMA((len(LOADS),)),
+            pltpu.SemaphoreType.DMA((2 * SPLIT,)),
         ],
         compiler_params=pltpu.CompilerParams(
             vmem_limit_bytes=56 * 1024 * 1024, collective_id=0, has_side_effects=True
         ),
         name="slice_kernel",
-    )(
-        motion,
-        line_mask,
-        planes,
-        psf_phase,
-        row_table,
-        column_table,
-        coil_planes,
-        encode_table,
-        decode_table,
-    )
+    )(motion, line_mask, *loads)
     return jnp.transpose(total, (2, 0, 1))
 
 
@@ -576,7 +785,7 @@
     lines = image.shape[0]
     width = image.shape[2]
     readout = psf_phase.shape[1]
-    if lines == NY and lax.axis_size("shot") == 2:
+    if lines == NY and lax.axis_size("shot") == 2 and fits(lines, width, readout):
         return whole_slice(image, coil_maps, psf_phase, line_mask, motion)
     devices = lax.axis_size("space")
     device_rank = lax.axis_index("space")

time: 34.4 us -> 26 us (0.76)
  Pallas kernels: 32.5 us -> 21.9 us
  local copies, waits for them, and re-layouts: 1.77 us -> 3.83 us
    pallas_call x1, Pallas kernels: 32.5 us -> 21.9 us  [whole_slice(): pl.pallas_call(slice_kernel, out_shape=jax.ShapeDtypeStruct((2, width, he...]
    unnamed x1 -> x2, local copies, waits for them, and re-layouts: 1.77 us -> 3.83 us
where the time goes in v1:
time: 26 us; the launch traced here: 25.8 us
  Pallas kernels  21.9 us (84%)
  local copies, waits for them, and re-layouts  3.83 us (15%)
    pallas_call x1, Pallas kernels, whole_slice(): pl.pallas_call(slice_kernel, out_shape=jax.ShapeDtypeStruct((2, width, he...  21.9 us
    unnamed x2, local copies, waits for them, and re-layouts  3.83 us

profile of v1, /device:TPU:9, one launch (start us, length us, event | category | flops | bytes accessed | tf_op | source)
XLA Modules:
  0.0 25.8 jit_solution(3689481643918878707)
XLA Ops:
  0.0 2.1 %copy.18 = f32[200,576]{0,1:T(8,128)} copy(f32[200,576]{1,0:T(8,128)} %param.19) | data formatting | bytes 921600 | tf_op args[2]
  2.1 21.9 %slice_kernel.1 = f32[2,192,200]{2,1,0:T(8,128)} custom-call(s32[1,3]{1,0:T(1,128)} %motion_ref.1, s32[1,200]{1,0:T(1,128)} %mask_ref.1, f32[2,192,200]{2,1,0:T(8,128)} %bitcast.7, bf16[2,192,192]{2,1,0:T(8,128)(2,1)} %constant.24.clone.refs_1_, bf16[2,192,192]{2,1,0:T(8,128)(2,1)} %constant.25.clone.refs_2_, f32[576,200]{1,0:T(8,128)} %bitcast.5, ...), custom_call_target="tpu_custom_call" | custom-call | tf_op jit(solution)/shard_map/slice_kernel/pallas_call | solution.py:750
  24.0 1.8 %copy.20 = f32[200,2,192]{0,2,1:T(8,128)} copy(f32[200,2,192]{0,2,1:T(8,128)} %bitcast.6) | data formatting | bytes 614400

commit v2 on v1

--- a/solution.py
+++ b/solution.py
@@ -310,10 +310,13 @@
     line_right[:height, HALF : HALF + middle] = sine[:, :middle]
     line_right[TALL : TALL + height, HALF : HALF + middle] = -cosine[:, :middle]
 
-    spreader = np.zeros((TALL, TALL))
-    spreader[lines, spread] = 1.0
-    mirror = np.zeros((readout // 2, readout // 2))
-    mirror[np.arange(readout // 2), -np.arange(readout // 2) % (readout // 2)] = 1.0
+    half = readout // 2
+    at = np.arange(half)
+    ahead = np.zeros((half, -(-half // HALF) * HALF))
+    ahead[at, at] = 1.0
+    first = half // HALF * HALF
+    behind = np.zeros((half, readout - first))
+    behind[at, half + -at % half - first] = 1.0
 
     def narrow(table):
         return table.astype(np.float32).astype(jnp.bfloat16)
@@ -325,8 +328,8 @@
         column_spread_back=split_table(padded.T),
         column_spread=split_table(padded),
         column_back=split_table(natural.T),
-        spreader=narrow(spreader),
-        mirror=narrow(mirror),
+        ahead=narrow(ahead),
+        behind=narrow(behind),
         line_left=split_table(line_left),
         line_right=split_table(line_right),
         encode=narrow(spectrum),
@@ -371,14 +374,16 @@
 
 
 LOADS = (
+    "motion",
     "image",
     "row",
     "row_back",
+    "mask",
     "psf",
     "column",
     "column_spread_back",
-    "spreader",
-    "mirror",
+    "ahead",
+    "behind",
     "line_left",
     "line_right",
     "coil",
@@ -387,18 +392,20 @@
     "column_spread",
     "column_back",
 )
+EARLY = 6
 UNROLL = 4
 SPLIT = 2
 
 
-def slice_kernel(motion_ref, mask_ref, *refs):
+def slice_kernel(*refs):
     count = len(LOADS)
     sources = dict(zip(LOADS, refs[:count]))
-    out_ref = refs[count]
-    held = dict(zip(LOADS, refs[count + 1 : 2 * count + 1]))
+    own_ref, other_s = refs[count : count + 2]
+    held = dict(zip(LOADS, refs[count + 2 : 2 * count + 2]))
     (
         image_s,
         psf_s,
+        wave_s,
         tail_s,
         coil_s,
         mask_s,
@@ -412,12 +419,11 @@
         fold_s,
         unwaved_s,
         sum_s,
-        other_s,
         load_sems,
         link_sems,
-    ) = refs[2 * count + 1 :]
+    ) = refs[2 * count + 2 :]
     _, width, height = sources["image"].shape
-    readout = sources["psf"].shape[0]
+    readout = sources["psf"].shape[1]
     coils = sources["coil"].shape[0]
     half_width, half_readout = width // 2, readout // 2
     tail = height - HALF
@@ -427,7 +433,7 @@
         name: pltpu.make_async_copy(sources[name], held[name], load_sems.at[at])
         for at, name in enumerate(LOADS)
     }
-    for name in LOADS:
+    for name in LOADS[:EARLY]:
         copies[name].start()
     partner = {"shot": 1 - lax.axis_index("shot")}
     barrier = pltpu.get_barrier_semaphore()
@@ -435,6 +441,14 @@
         barrier, inc=1, device_id=partner, device_id_type=pl.DeviceIdType.MESH
     )
 
+    image_s[...] = jnp.zeros_like(image_s)
+    psf_s[...] = jnp.zeros_like(psf_s)
+    tail_s[...] = jnp.zeros_like(tail_s)
+    mask_s[...] = jnp.zeros_like(mask_s)
+    sum_s[...] = jnp.zeros_like(sum_s)
+    wave_s[...] = jnp.zeros_like(wave_s)
+    copies["motion"].wait()
+    motion_ref = held["motion"]
     theta = (motion_ref[0, 0].astype(jnp.float32) - (LEVELS - 1) / 2.0) * ANGLE_STEP
     shift_x = (motion_ref[0, 1].astype(jnp.float32) - (LEVELS - 1) / 2.0) * SHIFT_STEP
     shift_y = (motion_ref[0, 2].astype(jnp.float32) - (LEVELS - 1) / 2.0) * SHIFT_STEP
@@ -537,62 +551,85 @@
             )
         return column_apply(tables[1], out[0]), column_apply(tables[1], out[1])
 
-    image_s[...] = jnp.zeros_like(image_s)
-    psf_s[:, HALF:] = jnp.zeros((readout, TALL - HALF), jnp.float32)
-    tail_s[...] = jnp.zeros_like(tail_s)
-    mask_s[...] = jnp.zeros_like(mask_s)
-    mask_s[:, :height] = floats(mask_ref[...])
     row_phase(0, False, shift_x)
-    column_phase()
-    row_phase(1, True, 0.0)
     copies["image"].wait()
     copies["row"].wait()
     copies["row_back"].wait()
+    for name in LOADS[EARLY:]:
+        copies[name].start()
     image_s[:, :, :height] = held["image"][...]
     real, imag = shear_rows(image_s[0], image_s[1], 0, 1.0)
+    column_phase()
+    row_phase(1, True, 0.0)
     copies["column"].wait()
     copies["column_spread_back"].wait()
     real, imag = shear_columns(real, imag, ("column", "column_spread_back"), 1.0)
 
     copies["psf"].wait()
-    psf_s[:, :height] = held["psf"][...]
-    copies["spreader"].wait()
-    copies["mirror"].wait()
-    for at in range(0, readout, 32):
-        turn = cos_sin_of_half(psf_s[at : at + 32] * 0.5)
+    middle = height // 2
+    psf_s[:middle] = held["psf"][:middle]
+    psf_s[HALF : HALF + middle] = held["psf"][middle:]
+    for start in (0, HALF):
+        for at in range(start, start + round_up(middle, 16), 16):
+            turn = cos_sin_of_half(psf_s[at : at + 16] * 0.5)
+            for which in range(2):
+                wave_s[which, at : at + 16] = turn[which].astype(jnp.bfloat16)
+    copies["ahead"].wait()
+    copies["behind"].wait()
+    for side, name in enumerate(("ahead", "behind")):
+        wide = held[name].shape[1]
         for which in range(2):
-            value = mxu(turn[which].astype(jnp.bfloat16), held["spreader"][...])
-            value = value.astype(jnp.bfloat16)
+            if side:
+                wave = wave_s[which, :, readout - wide :]
+            else:
+                wave = wave_s[which, :, :wide]
+            value = lax.dot_general(
+                held[name][...],
+                wave,
+                (((1,), (1,)), ((), ())),
+                preferred_element_type=jnp.float32,
+            ).astype(jnp.bfloat16)
+            rows = slice(side * half_readout, (side + 1) * half_readout)
             for part in range(2):
-                turn_s[which, part, at : at + 32] = value[:, part * HALF : (part + 1) * HALF]
-    behind = jnp.concatenate(
-        [turn_s[which, part, half_readout:] for which in range(2) for part in range(2)], 1
-    )
-    behind = mxu(held["mirror"][...], behind).astype(jnp.bfloat16)
-    for at in range(4):
-        turn_s[at // 2, at % 2, half_readout:] = behind[:, at * HALF : (at + 1) * HALF]
-
+                turn_s[which, part, rows] = value[:, part * HALF : (part + 1) * HALF]
+
+    copies["mask"].wait()
+    mask_s[:, :height] = floats(held["mask"][...])
     copies["line_left"].wait()
     copies["line_right"].wait()
     mask = mask_s[...]
     mask = jnp.concatenate([mask, mask], 1)
     odd_line = iota(mask.shape, 1) % 2
+    direct, crossed = [], []
     for parity in range(2):
         chosen = jnp.where(odd_line == parity, mask, 0.0)
         left = [
             (floats(held["line_left"][part]) * chosen).astype(jnp.bfloat16) for part in range(2)
         ]
         table = mxu_split(left, (held["line_right"][0], held["line_right"][1]))
-        direct, crossed = table[:, :HALF], table[:, HALF:]
-        table_s[parity, :HALF] = table.astype(jnp.bfloat16)
-        table_s[parity, HALF:, :HALF] = (-crossed).astype(jnp.bfloat16)
-        table_s[parity, HALF:, HALF:] = direct.astype(jnp.bfloat16)
+        direct.append(table[:, :HALF])
+        crossed.append(table[:, HALF:])
+    diagonal = iota((HALF, HALF), 0) == iota((HALF, HALF), 1)
+
+    def rounded(value):
+        return floats(value.astype(jnp.bfloat16))
+
+    whole = rounded(direct[0] + direct[1])
+    even = rounded(whole + direct[0]) - whole
+    direct = [
+        jnp.where(diagonal, even, direct[0]),
+        jnp.where(diagonal, whole - even, direct[1]),
+    ]
+    for parity in range(2):
+        table_s[parity, :HALF, :HALF] = direct[parity].astype(jnp.bfloat16)
+        table_s[parity, :HALF, HALF:] = crossed[parity].astype(jnp.bfloat16)
+        table_s[parity, HALF:, :HALF] = (-crossed[parity]).astype(jnp.bfloat16)
+        table_s[parity, HALF:, HALF:] = direct[parity].astype(jnp.bfloat16)
 
     real, imag = shear_rows(real, imag, 1, 1.0)
     for part in range(2):
         rotated_s[part, 0] = real[:, part * HALF : (part + 1) * HALF]
         rotated_s[part, 1] = imag[:, part * HALF : (part + 1) * HALF]
-    sum_s[...] = jnp.zeros_like(sum_s)
 
     copies["coil"].wait()
     copies["encode"].wait()
@@ -610,24 +647,21 @@
             spread.append((low, high))
             coil_s[slot, at, 0] = low
             coil_s[slot, at, 1] = high
+        reals, imags = [], []
         for part in range(2):
             real, imag = rotated_s[part, 0], rotated_s[part, 1]
             coil_real, coil_imag = spread[0][part], spread[1][part]
-            coil_image_s[part] = (coil_real * real - coil_imag * imag).astype(jnp.bfloat16)
-            coil_image_s[2 + part] = (coil_real * imag + coil_imag * real).astype(jnp.bfloat16)
-
-    def head(value):
-        return value[:16]
+            reals.append((coil_real * real - coil_imag * imag).astype(jnp.bfloat16))
+            imags.append((coil_real * imag + coil_imag * real).astype(jnp.bfloat16))
+        return reals + imags
 
     first = iota((16, HALF), 0) == 0
 
     def joined(chosen, value):
         return jnp.concatenate([jnp.where(first, chosen[:16], value[:16]), value[16:]], 0)
 
-    def encode():
-        spectra = mxu(
-            held["encode"][...], jnp.concatenate([coil_image_s[at] for at in range(4)], 1)
-        )
+    def encode(coil_image):
+        spectra = mxu(held["encode"][...], jnp.concatenate(coil_image, 1))
         waved = []
         for part in range(2):
             lanes = slice(part * HALF, (part + 1) * HALF)
@@ -644,18 +678,21 @@
                 rows = slice(side * half_readout, (side + 1) * half_readout)
                 cosine, sine = turn_s[0, part, rows], turn_s[1, part, rows]
                 waved.append((real * cosine - imag * sine, real * sine + imag * cosine))
-        for side in range(2):
-            rows = slice(side * half_readout, (side + 1) * half_readout)
-            for at in range(2):
-                low, high = waved[side][at], waved[2 + side][at]
-                fold_s[0, at, rows] = low + high
-                fold_s[1, at, rows] = low - high
-
-    def project():
-        even, odd = [
-            mxu(jnp.concatenate([fold_s[at, 0], fold_s[at, 1]], 1), table_s[at])
-            for at in range(2)
-        ]
+        folded = []
+        for sign in (1, -1):
+            sides = []
+            for side in range(2):
+                pieces = []
+                for at in range(2):
+                    low, high = waved[side][at], waved[2 + side][at]
+                    pieces.append(low + high if sign > 0 else low - high)
+                sides.append(pieces)
+            folded.append([jnp.concatenate([sides[0][at], sides[1][at]], 0) for at in range(2)])
+        return folded
+
+    def project(folded):
+        even, odd = [mxu(jnp.concatenate(folded[at], 1), table_s[at]) for at in range(2)]
+        unwaved = [None] * 4
         for part, value in enumerate((even + odd, even - odd)):
             value = value.astype(jnp.bfloat16)
             real, imag = value[:, :HALF], value[:, HALF:]
@@ -663,13 +700,24 @@
             unreal, unimag = real * cosine + imag * sine, imag * cosine - real * sine
             plus_real, minus_real = unreal[:half_readout], unreal[half_readout:]
             plus_imag, minus_imag = unimag[:half_readout], unimag[half_readout:]
-            unwaved_s[part, :half_readout] = joined(plus_real, plus_real + minus_real)
-            unwaved_s[2 + part, :half_readout] = joined(plus_imag, plus_imag + minus_imag)
-            unwaved_s[part, half_readout:] = joined(minus_real, minus_imag - plus_imag)
-            unwaved_s[2 + part, half_readout:] = joined(minus_imag, plus_real - minus_real)
-
-    def decode(slot):
-        back = mxu(held["decode"][...], jnp.concatenate([unwaved_s[at] for at in range(4)], 1))
+            unwaved[part] = jnp.concatenate(
+                [
+                    joined(plus_real, plus_real + minus_real),
+                    joined(minus_real, minus_imag - plus_imag),
+                ],
+                0,
+            )
+            unwaved[2 + part] = jnp.concatenate(
+                [
+                    joined(plus_imag, plus_imag + minus_imag),
+                    joined(minus_imag, plus_real - minus_real),
+                ],
+                0,
+            )
+        return unwaved
+
+    def decode(unwaved, slot):
+        back = mxu(held["decode"][...], jnp.concatenate(unwaved, 1))
         for part in range(2):
             real = back[:, part * HALF : (part + 1) * HALF]
             imag = back[:, TALL + part * HALF : TALL + (part + 1) * HALF]
@@ -677,31 +725,41 @@
             sum_s[0, part] += coil_real * real + coil_imag * imag
             sum_s[1, part] += coil_real * imag - coil_imag * real
 
-    multiply(0, 0)
-    encode()
-    multiply(1, 1)
-    project()
-    encode()
-    multiply(2, 2)
+    def run(start, many, entering, leaving, begin):
+        if entering:
+            coil_image = [coil_image_s[at] for at in range(4)]
+            folded = [[fold_s[at, piece] for piece in range(2)] for at in range(2)]
+            unwaved = [unwaved_s[at] for at in range(4)]
+        else:
+            coil_image = multiply(start, 0)
+            folded = encode(coil_image)
+            coil_image = multiply(start + 1, 1)
+            unwaved = project(folded)
+            folded = encode(coil_image)
+            coil_image = multiply(start + 2, 2)
+        for inner in range(many):
+            decode(unwaved, (begin + inner) % UNROLL)
+            if inner + 1 < many or leaving:
+                unwaved = project(folded)
+            if inner + 2 < many or leaving:
+                folded = encode(coil_image)
+            if inner + 3 < many or leaving:
+                coil_image = multiply(start + inner + 3, (begin + inner + 3) % UNROLL)
+        if leaving:
+            for at in range(4):
+                coil_image_s[at] = coil_image[at]
+                unwaved_s[at] = unwaved[at]
+                fold_s[at // 2, at % 2] = folded[at // 2][at % 2]
 
     def step(at, carry):
-        for inner in range(UNROLL):
-            decode(inner)
-            project()
-            encode()
-            multiply(at * UNROLL + inner + 3, (inner + 3) % UNROLL)
+        run((at + 1) * UNROLL, UNROLL, True, True, 0)
         return carry
 
-    rounds = (coils - 3) // UNROLL
-    lax.fori_loop(0, rounds, step, 0)
-    for coil in range(rounds * UNROLL, coils):
-        decode(coil % UNROLL)
-        if coil + 1 < coils:
-            project()
-        if coil + 2 < coils:
-            encode()
-        if coil + 3 < coils:
-            multiply(coil + 3, (coil + 3) % UNROLL)
+    rounds = (coils - 1) // UNROLL
+    run(0, UNROLL, False, True, 0)
+    if rounds > 1:
+        lax.fori_loop(0, rounds - 1, step, 0)
+    run(rounds * UNROLL, coils - rounds * UNROLL, True, False, 0)
 
     copies["column_spread"].wait()
     copies["column_back"].wait()
@@ -715,10 +773,10 @@
     for at in range(SPLIT):
         span = (at * size, (at + 1) * size)
         for part in range(2):
-            image_s[part, span[0] : span[1]] = row_apply("row_back", halves[part], span)
+            own_ref[part, span[0] : span[1]] = row_apply("row_back", halves[part], span)
         links.append(
             pltpu.make_async_remote_copy(
-                src_ref=image_s.at[:, pl.ds(span[0], size)],
+                src_ref=own_ref.at[:, pl.ds(span[0], size)],
                 dst_ref=other_s.at[:, pl.ds(span[0], size)],
                 send_sem=link_sems.at[2 * at],
                 recv_sem=link_sems.at[2 * at + 1],
@@ -729,10 +787,13 @@
         links[at].start()
     for at in range(SPLIT):
         links[at].wait_recv()
-        rows = slice(at * size, (at + 1) * size)
-        out_ref[:, rows] = (image_s[:, rows] + other_s[:, rows])[:, :, :height]
     for at in range(SPLIT):
         links[at].wait_send()
+
+
+def add_kernel(own_ref, other_ref, out_ref):
+    height = out_ref.shape[2]
+    out_ref[...] = (own_ref[...] + other_ref[...])[:, :, :height]
 
 
 def whole_slice(image, coil_maps, psf_phase, line_mask, motion):
@@ -743,19 +804,23 @@
     }
     arrays["image"] = jnp.transpose(image, (1, 2, 0))
     arrays["coil"] = jnp.transpose(coil_maps, (0, 2, 3, 1))
-    arrays["psf"] = jnp.transpose(psf_phase)
+    arrays["psf"] = psf_phase
+    arrays["mask"] = line_mask
+    arrays["motion"] = motion
     loads = [arrays[name] for name in LOADS]
     vmem = pl.BlockSpec(memory_space=pltpu.VMEM)
     anywhere = pl.BlockSpec(memory_space=pl.ANY)
     total = pl.pallas_call(
         slice_kernel,
-        out_shape=jax.ShapeDtypeStruct((2, width, height), jnp.float32),
-        in_specs=[pl.BlockSpec(memory_space=pltpu.SMEM), vmem] + [anywhere] * len(LOADS),
-        out_specs=vmem,
-        scratch_shapes=[pltpu.VMEM(value.shape, value.dtype) for value in loads]
+        out_shape=[pltpu.VMEM((2, width, TALL), jnp.float32)] * 2,
+        in_specs=[anywhere] * len(LOADS),
+        out_specs=[vmem] * 2,
+        scratch_shapes=[pltpu.SMEM(motion.shape, motion.dtype)]
+        + [pltpu.VMEM(value.shape, value.dtype) for value in loads[1:]]
         + [
             pltpu.VMEM((2, width, TALL), jnp.float32),
-            pltpu.VMEM((readout, TALL), jnp.float32),
+            pltpu.VMEM((TALL, readout), jnp.float32),
+            pltpu.VMEM((2, TALL, readout), jnp.bfloat16),
             pltpu.VMEM((2, width, HALF), jnp.float32),
             pltpu.VMEM((UNROLL, 2, 2, width, HALF), jnp.float32),
             pltpu.VMEM((1, TALL), jnp.float32),
@@ -769,7 +834,6 @@
             pltpu.VMEM((2, 2, readout, HALF), jnp.bfloat16),
             pltpu.VMEM((4, readout, HALF), jnp.bfloat16),
             pltpu.VMEM((2, 2, width, HALF), jnp.float32),
-            pltpu.VMEM((2, width, TALL), jnp.float32),
             pltpu.SemaphoreType.DMA((len(LOADS),)),
             pltpu.SemaphoreType.DMA((2 * SPLIT,)),
         ],
@@ -777,8 +841,15 @@
             vmem_limit_bytes=56 * 1024 * 1024, collective_id=0, has_side_effects=True
         ),
         name="slice_kernel",
-    )(motion, line_mask, *loads)
-    return jnp.transpose(total, (2, 0, 1))
+    )(*loads)
+    result = pl.pallas_call(
+        add_kernel,
+        out_shape=jax.ShapeDtypeStruct((2, width, height), jnp.float32),
+        in_specs=[vmem] * 2,
+        out_specs=vmem,
+        name="add_kernel",
+    )(*[pltpu.with_memory_space_constraint(value, pltpu.VMEM) for value in total])
+    return jnp.transpose(result, (2, 0, 1))
 
 
 def on_device(image, coil_maps, psf_phase, line_mask, motion):

time: 26 us -> 20.2 us (0.78)
  local copies, waits for them, and re-layouts: 3.83 us -> 0 us
  Pallas kernels: 21.9 us -> 20 us
    unnamed x2 -> x0, local copies, waits for them, and re-layouts: 3.83 us -> none
    pallas_call x1 -> x2, Pallas kernels: 21.9 us -> 20 us  [the longest x1 19.3 us: whole_slice(): pl.pallas_call(slice_kernel, out_shape=[pltpu.VMEM((2, width, TALL), jnp....]
where the time goes in v2:
time: 20.2 us; the launch traced here: 20.1 us
  Pallas kernels  20 us (99%)
    pallas_call x1, Pallas kernels, whole_slice(): pl.pallas_call(slice_kernel, out_shape=[pltpu.VMEM((2, width, TALL), jnp....  19.3 us
    pallas_call x1, Pallas kernels, whole_slice(): pl.pallas_call(add_kernel, out_shape=jax.ShapeDtypeStruct((2, width, heig...  0.79 us

profile of v2, /device:TPU:9, one launch (start us, length us, event | category | flops | bytes accessed | tf_op | source)
XLA Modules:
  0.0 20.1 jit_solution(6985731472757342919)
XLA Ops:
  0.0 19.3 %slice_kernel.1 = (f32[2,192,256]{2,1,0:T(8,128)S(1)}, f32[2,192,256]{2,1,0:T(8,128)S(1)}) custom-call(s32[1,3]{1,0:T(1,128)} %refs_0_.1, f32[2,192,200]{2,1,0:T(8,128)} %bitcast.4, bf16[2,192,192]{2,1,0:T(8,128)(2,1)} %constant.24.clone.refs_2_, bf16[2,192,192]{2,1,0:T(8,128)(2,1)} %constant.25.clone.refs_3_, s32[1,200]{1,0:T(1,128)} %refs_4_.1, ...), custom_call_target="tpu_custom_call" | custom-call | tf_op jit(solution)/shard_map/slice_kernel/pallas_call | solution.py:813
  19.3 0.8 %add_kernel.1 = f32[2,192,200]{2,1,0:T(8,128)} custom-call(f32[2,192,256]{2,1,0:T(8,128)S(1)} %get-tuple-element.7.own_ref, f32[2,192,256]{2,1,0:T(8,128)S(1)} %get-tuple-element.8.other_ref), custom_call_target="tpu_custom_call" | custom-call | tf_op jit(solution)/shard_map/add_kernel/pallas_call | solution.py:845

commit v3 on v2

--- a/solution.py
+++ b/solution.py
@@ -375,13 +375,13 @@
 
 LOADS = (
     "motion",
+    "psf",
     "image",
     "row",
     "row_back",
-    "mask",
-    "psf",
     "column",
     "column_spread_back",
+    "mask",
     "ahead",
     "behind",
     "line_left",
@@ -392,7 +392,8 @@
     "column_spread",
     "column_back",
 )
-EARLY = 6
+EARLY = 7
+LATE = 12
 UNROLL = 4
 SPLIT = 2
 
@@ -552,19 +553,8 @@
         return column_apply(tables[1], out[0]), column_apply(tables[1], out[1])
 
     row_phase(0, False, shift_x)
-    copies["image"].wait()
-    copies["row"].wait()
-    copies["row_back"].wait()
-    for name in LOADS[EARLY:]:
-        copies[name].start()
-    image_s[:, :, :height] = held["image"][...]
-    real, imag = shear_rows(image_s[0], image_s[1], 0, 1.0)
     column_phase()
     row_phase(1, True, 0.0)
-    copies["column"].wait()
-    copies["column_spread_back"].wait()
-    real, imag = shear_columns(real, imag, ("column", "column_spread_back"), 1.0)
-
     copies["psf"].wait()
     middle = height // 2
     psf_s[:middle] = held["psf"][:middle]
@@ -574,8 +564,16 @@
             turn = cos_sin_of_half(psf_s[at : at + 16] * 0.5)
             for which in range(2):
                 wave_s[which, at : at + 16] = turn[which].astype(jnp.bfloat16)
-    copies["ahead"].wait()
-    copies["behind"].wait()
+    for name in LOADS[2:EARLY]:
+        copies[name].wait()
+    for name in LOADS[EARLY:]:
+        copies[name].start()
+    image_s[:, :, :height] = held["image"][...]
+    real, imag = shear_rows(image_s[0], image_s[1], 0, 1.0)
+    real, imag = shear_columns(real, imag, ("column", "column_spread_back"), 1.0)
+
+    for name in LOADS[EARLY:LATE]:
+        copies[name].wait()
     for side, name in enumerate(("ahead", "behind")):
         wide = held[name].shape[1]
         for which in range(2):
@@ -593,10 +591,7 @@
             for part in range(2):
                 turn_s[which, part, rows] = value[:, part * HALF : (part + 1) * HALF]
 
-    copies["mask"].wait()
     mask_s[:, :height] = floats(held["mask"][...])
-    copies["line_left"].wait()
-    copies["line_right"].wait()
     mask = mask_s[...]
     mask = jnp.concatenate([mask, mask], 1)
     odd_line = iota(mask.shape, 1) % 2
@@ -631,9 +626,9 @@
         rotated_s[part, 0] = real[:, part * HALF : (part + 1) * HALF]
         rotated_s[part, 1] = imag[:, part * HALF : (part + 1) * HALF]
 
-    copies["coil"].wait()
-    copies["encode"].wait()
-    copies["decode"].wait()
+
+    for name in LOADS[LATE:]:
+        copies[name].wait()
 
     def multiply(coil, slot):
         early = iota((width, HALF), 1) < ahead
@@ -738,11 +733,12 @@
             folded = encode(coil_image)
             coil_image = multiply(start + 2, 2)
         for inner in range(many):
-            decode(unwaved, (begin + inner) % UNROLL)
+            old_unwaved, old_folded, old_image = unwaved, folded, coil_image
+            decode(old_unwaved, (begin + inner) % UNROLL)
             if inner + 1 < many or leaving:
-                unwaved = project(folded)
+                unwaved = project(old_folded)
             if inner + 2 < many or leaving:
-                folded = encode(coil_image)
+                folded = encode(old_image)
             if inner + 3 < many or leaving:
                 coil_image = multiply(start + inner + 3, (begin + inner + 3) % UNROLL)
         if leaving:
@@ -761,8 +757,6 @@
         lax.fori_loop(0, rounds - 1, step, 0)
     run(rounds * UNROLL, coils - rounds * UNROLL, True, False, 0)
 
-    copies["column_spread"].wait()
-    copies["column_back"].wait()
     real, imag = [jnp.concatenate([sum_s[at, 0], sum_s[at, 1]], 1) for at in range(2)]
     real, imag = shear_rows(real, imag, 1, -1.0)
     real, imag = shear_columns(real, imag, ("column_spread", "column_back"), -1.0)

time: 20.2 us -> 19.7 us (0.975)
  Pallas kernels: 20 us -> 19.5 us
    pallas_call x1, Pallas kernels: 19.3 us -> 18.8 us  [whole_slice(): pl.pallas_call(slice_kernel, out_shape=[pltpu.VMEM((2, width, TALL), jnp....]
where the time goes in v3:
time: 19.7 us; the launch traced here: 19.6 us
  Pallas kernels  19.5 us (99%)
    pallas_call x1, Pallas kernels, whole_slice(): pl.pallas_call(slice_kernel, out_shape=[pltpu.VMEM((2, width, TALL), jnp....  18.8 us
    pallas_call x1, Pallas kernels, whole_slice(): pl.pallas_call(add_kernel, out_shape=jax.ShapeDtypeStruct((2, width, heig...  0.79 us

profile of v3, /device:TPU:9, one launch (start us, length us, event | category | flops | bytes accessed | tf_op | source)
XLA Modules:
  0.0 19.6 jit_solution(902988011453413286)
XLA Ops:
  0.0 18.8 %slice_kernel.1 = (f32[2,192,256]{2,1,0:T(8,128)S(1)}, f32[2,192,256]{2,1,0:T(8,128)S(1)}) custom-call(s32[1,3]{1,0:T(1,128)} %refs_0_.1, f32[200,576]{1,0:T(8,128)} %refs_1_.1, f32[2,192,200]{2,1,0:T(8,128)} %bitcast.4, bf16[2,192,192]{2,1,0:T(8,128)(2,1)} %constant.24.clone.refs_3_, bf16[2,192,192]{2,1,0:T(8,128)(2,1)} %constant.25.clone.refs_4_, ...), custom_call_target="tpu_custom_call" | custom-call | tf_op jit(solution)/shard_map/slice_kernel/pallas_call | solution.py:807
  18.8 0.8 %add_kernel.1 = f32[2,192,200]{2,1,0:T(8,128)} custom-call(f32[2,192,256]{2,1,0:T(8,128)S(1)} %get-tuple-element.7.own_ref, f32[2,192,256]{2,1,0:T(8,128)S(1)} %get-tuple-element.8.other_ref), custom_call_target="tpu_custom_call" | custom-call | tf_op jit(solution)/shard_map/add_kernel/pallas_call | solution.py:839

commit v4 on v3

--- a/solution.py
+++ b/solution.py
@@ -556,6 +556,8 @@
     column_phase()
     row_phase(1, True, 0.0)
     copies["psf"].wait()
+    for name in LOADS[EARLY:]:
+        copies[name].start()
     middle = height // 2
     psf_s[:middle] = held["psf"][:middle]
     psf_s[HALF : HALF + middle] = held["psf"][middle:]
@@ -566,8 +568,6 @@
                 wave_s[which, at : at + 16] = turn[which].astype(jnp.bfloat16)
     for name in LOADS[2:EARLY]:
         copies[name].wait()
-    for name in LOADS[EARLY:]:
-        copies[name].start()
     image_s[:, :, :height] = held["image"][...]
     real, imag = shear_rows(image_s[0], image_s[1], 0, 1.0)
     real, imag = shear_columns(real, imag, ("column", "column_spread_back"), 1.0)

time: 19.7 us -> 19.5 us (0.990)
  Pallas kernels: 19.5 us -> 19.3 us
    pallas_call x1, Pallas kernels: 18.8 us -> 18.5 us  [whole_slice(): pl.pallas_call(slice_kernel, out_shape=[pltpu.VMEM((2, width, TALL), jnp....]
where the time goes in v4:
time: 19.5 us; the launch traced here: 19.3 us
  Pallas kernels  19.3 us (99%)
    pallas_call x1, Pallas kernels, whole_slice(): pl.pallas_call(slice_kernel, out_shape=[pltpu.VMEM((2, width, TALL), jnp....  18.5 us
    pallas_call x1, Pallas kernels, whole_slice(): pl.pallas_call(add_kernel, out_shape=jax.ShapeDtypeStruct((2, width, heig...  0.79 us

profile of v4, /device:TPU:9, one launch (start us, length us, event | category | flops | bytes accessed | tf_op | source)
XLA Modules:
  0.0 19.3 jit_solution(2302169010897803823)
XLA Ops:
  0.0 18.5 %slice_kernel.1 = (f32[2,192,256]{2,1,0:T(8,128)S(1)}, f32[2,192,256]{2,1,0:T(8,128)S(1)}) custom-call(s32[1,3]{1,0:T(1,128)} %refs_0_.1, f32[200,576]{1,0:T(8,128)} %refs_1_.1, f32[2,192,200]{2,1,0:T(8,128)} %bitcast.4, bf16[2,192,192]{2,1,0:T(8,128)(2,1)} %constant.24.clone.refs_3_, bf16[2,192,192]{2,1,0:T(8,128)(2,1)} %constant.25.clone.refs_4_, ...), custom_call_target="tpu_custom_call" | custom-call | tf_op jit(solution)/shard_map/slice_kernel/pallas_call | solution.py:807
  18.5 0.8 %add_kernel.1 = f32[2,192,200]{2,1,0:T(8,128)} custom-call(f32[2,192,256]{2,1,0:T(8,128)S(1)} %get-tuple-element.7.own_ref, f32[2,192,256]{2,1,0:T(8,128)S(1)} %get-tuple-element.8.other_ref), custom_call_target="tpu_custom_call" | custom-call | tf_op jit(solution)/shard_map/add_kernel/pallas_call | solution.py:839
